TPU v7x, 32 devices: a whole 2x2x4 slice. The times are simulated.
32 devices in a mesh: wide: 8 (over z, y), narrow: 4 (over x, core).
Axes of the slice: x: 2, y: 2, z: 4, core: 2. Of those that a mesh axis runs over, the one named last changes fastest.
Arguments:
- layer_in: bfloat16 [8, 512, 1536], P('wide', 'narrow'), may hold values from -6 to 6
- lengths: int32 [8, 8], P('wide'), may hold values from 1 to 256, 512 in all within a row
- w_qkv: bfloat16 [1536, 2048], P(('wide', 'narrow')), may hold values from -0.15625 to 0.15625
- b_qkv: bfloat16 [2048], P(('wide', 'narrow')), may hold values from -3 to 3
- w_out: bfloat16 [1536, 1536], P(None, ('wide', 'narrow')), may hold values from -0.625 to 0.625
- norm1_gain: bfloat16 [1536], P(('wide', 'narrow')), may hold values from 0.099609375 to 1.8984375
- norm2_gain: bfloat16 [1536], P(('wide', 'narrow')), may hold values from 0.099609375 to 1.8984375
- w_gate: bfloat16 [1536, 8960], P('wide', 'narrow'), may hold values from -0.15625 to 0.15625
- w_up: bfloat16 [1536, 8960], P('wide', 'narrow'), may hold values from -0.15625 to 0.15625
- w_down: bfloat16 [8960, 1536], P('narrow', 'wide'), may hold values from -0.0625 to 0.0625
- grad_out: bfloat16 [8, 512, 1536], P('wide', 'narrow'), may hold values from -6 to 6
Outputs:
- layer_out: bfloat16 [8, 512, 1536], P('wide', 'narrow')
- grad_in: float32 [8, 512, 1536], P('wide', 'narrow')
- grad_w_qkv: float32 [1536, 2048], P(('wide', 'narrow'))
- grad_b_qkv: float32 [2048], P(('wide', 'narrow'))
- grad_w_out: float32 [1536, 1536], P(None, ('wide', 'narrow'))
- grad_norm1: float32 [1536], P(('wide', 'narrow'))
- grad_norm2: float32 [1536], P(('wide', 'narrow'))
- grad_w_gate: float32 [1536, 8960], P('wide', 'narrow')
- grad_w_up: float32 [1536, 8960], P('wide', 'narrow')
- grad_w_down: float32 [8960, 1536], P('narrow', 'wide')
Inputs may be any that keep to these rules, and one draw needn't show every extreme that they name: In each pack the 8 lengths sum to 512, and one of them is 256.
All inputs are finite; a program needn't handle non-finite values.
Results may differ from a plain program's by a relative error of at most 0.02.
Values may be sent and summed in bfloat16 or wider, within the bound.
A program may use at most 192 MiB of HBM per device.

v0:
```python
import math
import jax
import jax.numpy as jnp
from jax import lax
from jax.sharding import PartitionSpec as P

QUERY_HEADS = 12
KEY_VALUE_HEADS = 2
HEAD_WIDTH = 128
EPSILON = 1e-06
ROPE_BASE = 10000.0
NEGATIVE_BIG = -1e30
HIGHEST = lax.Precision.HIGHEST


def rms_scale(value_rows, gain):
    return (
        value_rows
        * lax.rsqrt(jnp.mean(value_rows * value_rows, axis=-1, keepdims=True) + EPSILON)
        * gain
    )


def apply_rotation(value_rows, token_position):
    half_dim = value_rows.shape[-1] // 2
    freq = jnp.exp(
        jnp.arange(half_dim, dtype=jnp.float32)
        * (-2.0 * math.log(ROPE_BASE) / value_rows.shape[-1])
    )
    angle = token_position[:, None] * freq[None, :]
    cosine = jnp.cos(angle)[:, None, :]
    sine = jnp.sin(angle)[:, None, :]
    leading = value_rows[..., :half_dim]
    trailing = value_rows[..., half_dim:]
    return jnp.concatenate(
        [leading * cosine - trailing * sine, trailing * cosine + leading * sine], axis=-1
    )


def doc_layout(index, doc_lengths):
    ends = jnp.cumsum(doc_lengths)
    starts = ends - doc_lengths
    document_index = jnp.sum((index[:, None] >= ends[None, :]).astype(jnp.int32), axis=1)
    onehot = (
        document_index[:, None] == jnp.arange(doc_lengths.shape[0], dtype=jnp.int32)[None, :]
    ).astype(jnp.int32)
    token_position = index - jnp.sum(onehot * starts[None, :], axis=1)
    return (document_index, token_position.astype(jnp.float32))


def contract_rows(left, right):
    return lax.dot_general(
        left, right, (((0,), (0,)), ((), ())), preferred_element_type=jnp.float32
    )


def times_transposed(left, right):
    return lax.dot_general(
        left, right, (((1,), (1,)), ((), ())), preferred_element_type=jnp.float32
    )


def shards(
    layer_in, lengths, w_qkv, b_qkv, w_out, norm1_gain, norm2_gain, w_gate, w_up, w_down, grad_out
):
    hidden_in = layer_in[0].astype(jnp.float32)
    rows_per_shard = hidden_in.shape[0]
    narrow_count = lax.axis_size("narrow")
    first_row = lax.axis_index("narrow") * rows_per_shard
    pack_rows = rows_per_shard * narrow_count
    query_group = QUERY_HEADS // KEY_VALUE_HEADS
    query_total_width = QUERY_HEADS * HEAD_WIDTH
    key_total_width = KEY_VALUE_HEADS * HEAD_WIDTH
    scale = HEAD_WIDTH ** (-0.5)
    doc_lengths = lengths[0]
    local_index = first_row + jnp.arange(rows_per_shard, dtype=jnp.int32)
    local_doc, local_pos = doc_layout(local_index, doc_lengths)
    key_index = jnp.arange(pack_rows, dtype=jnp.int32)
    key_doc = doc_layout(key_index, doc_lengths)[0]
    wqkv_full, bias_full, wout_full, gain_one, gain_two = (
        lax.all_gather(w_qkv, ("wide", "narrow"), axis=0, tiled=True),
        lax.all_gather(b_qkv, ("wide", "narrow"), axis=0, tiled=True),
        lax.all_gather(w_out, ("wide", "narrow"), axis=1, tiled=True),
        lax.all_gather(norm1_gain, ("wide", "narrow"), axis=0, tiled=True),
        lax.all_gather(norm2_gain, ("wide", "narrow"), axis=0, tiled=True),
    )
    wgate_full, wup_full, wdown_full = (
        lax.all_gather(w_gate, "wide", axis=0, tiled=True),
        lax.all_gather(w_up, "wide", axis=0, tiled=True),
        lax.all_gather(w_down, "wide", axis=1, tiled=True),
    )
    gain_one = gain_one.astype(jnp.float32)
    gain_two = gain_two.astype(jnp.float32)
    normed_one = rms_scale(hidden_in, gain_one).astype(jnp.bfloat16)
    unrotated_projection = jnp.dot(
        normed_one, wqkv_full, preferred_element_type=jnp.float32
    ) + bias_full.astype(jnp.float32)
    pre_query = unrotated_projection[:, :query_total_width].reshape(
        rows_per_shard, QUERY_HEADS, HEAD_WIDTH
    )
    unrotated_key = unrotated_projection[
        :, query_total_width : query_total_width + key_total_width
    ].reshape(rows_per_shard, KEY_VALUE_HEADS, HEAD_WIDTH)

    def rotate_local(value_rows):
        return apply_rotation(value_rows, local_pos)

    rotated_query, query_back = jax.vjp(rotate_local, pre_query)
    key_rot, key_backward = jax.vjp(rotate_local, unrotated_key)
    query_rows = rotated_query.astype(jnp.bfloat16).reshape(
        rows_per_shard, KEY_VALUE_HEADS, query_group, HEAD_WIDTH
    )
    key_local = key_rot.reshape(rows_per_shard, key_total_width).astype(jnp.bfloat16)
    value_local = unrotated_projection[:, query_total_width + key_total_width :].astype(
        jnp.bfloat16
    )
    every_key_row, every_value_row = (
        lax.all_gather(key_local, "narrow", axis=0, tiled=True),
        lax.all_gather(value_local, "narrow", axis=0, tiled=True),
    )
    rows_per_block = min(512, pack_rows)
    count_of_blocks = pack_rows // rows_per_block
    blocked_keys = every_key_row.reshape(
        count_of_blocks, rows_per_block, KEY_VALUE_HEADS, HEAD_WIDTH
    )
    blocked_values = every_value_row.reshape(
        count_of_blocks, rows_per_block, KEY_VALUE_HEADS, HEAD_WIDTH
    )
    doc_blocks = key_doc.reshape(count_of_blocks, rows_per_block)
    index_blocks = key_index.reshape(count_of_blocks, rows_per_block)
    input_per_block = (blocked_keys, blocked_values, doc_blocks, index_blocks)

    def block_scores(key_block, doc_block, index_block):
        scores = (
            jnp.einsum("tkgd,skd->kgts", query_rows, key_block, preferred_element_type=jnp.float32)
            * scale
        )
        allowed = (local_doc[:, None] == doc_block[None, :]) & (
            index_block[None, :] <= local_index[:, None]
        )
        return (jnp.where(allowed, scores, NEGATIVE_BIG), allowed)

    def total_block(carry, inputs):
        running_max, running_sum = carry
        key_block, value_block, doc_block, index_block = inputs
        masked, allowed = block_scores(key_block, doc_block, index_block)
        new_max = jnp.maximum(running_max, jnp.max(masked, axis=-1))
        probs = jnp.where(allowed, jnp.exp(masked - new_max[..., None]), 0.0)
        running_sum = running_sum * jnp.exp(running_max - new_max) + jnp.sum(probs, axis=-1)
        return ((new_max, running_sum), None)

    start_carry = (
        jnp.full((KEY_VALUE_HEADS, query_group, rows_per_shard), NEGATIVE_BIG, jnp.float32),
        jnp.zeros((KEY_VALUE_HEADS, query_group, rows_per_shard), jnp.float32),
    )
    (final_max, final_sum), _ = lax.scan(total_block, start_carry, input_per_block)
    log_total = final_max + jnp.log(final_sum)

    def block_probs(key_block, doc_block, index_block):
        masked, allowed = block_scores(key_block, doc_block, index_block)
        return jnp.where(allowed, jnp.exp(masked - log_total[..., None]), 0.0)

    def block_forward_pass(weighted, inputs):
        key_block, value_block, doc_block, index_block = inputs
        probs_low = block_probs(key_block, doc_block, index_block).astype(jnp.bfloat16)
        weighted = weighted + jnp.einsum(
            "kgts,skd->kgtd", probs_low, value_block, preferred_element_type=jnp.float32
        )
        return (weighted, None)

    attn_heads, _ = lax.scan(
        block_forward_pass,
        jnp.zeros((KEY_VALUE_HEADS, query_group, rows_per_shard, HEAD_WIDTH), jnp.float32),
        input_per_block,
    )
    attn_low = (
        attn_heads.transpose(2, 0, 1, 3)
        .reshape(rows_per_shard, query_total_width)
        .astype(jnp.bfloat16)
    )
    middle = hidden_in + jnp.dot(attn_low, wout_full, preferred_element_type=jnp.float32)
    normed_two = rms_scale(middle, gain_two).astype(jnp.bfloat16)
    pack_normed = lax.all_gather(normed_two, "narrow", axis=0, tiled=True)
    gate = jnp.dot(pack_normed, wgate_full, preferred_element_type=jnp.float32)
    up_part = jnp.dot(pack_normed, wup_full, preferred_element_type=jnp.float32)
    sigmoid_gate = jax.nn.sigmoid(gate)
    activated = gate * sigmoid_gate
    hidden_act = (activated * up_part).astype(jnp.bfloat16)
    mixed = lax.psum_scatter(
        jnp.dot(hidden_act, wdown_full, preferred_element_type=jnp.float32).astype(jnp.bfloat16),
        "narrow",
        scatter_dimension=0,
        tiled=True,
    ).astype(jnp.float32)
    layer_out = (middle + mixed).astype(jnp.bfloat16)
    wgate_back, wup_back, wdown_back = (
        lax.all_gather(w_gate, "wide", axis=0, tiled=True),
        lax.all_gather(w_up, "wide", axis=0, tiled=True),
        lax.all_gather(w_down, "wide", axis=1, tiled=True),
    )
    cotangent = grad_out[0]
    pack_cotangent = lax.all_gather(cotangent, "narrow", axis=0, tiled=True)
    grad_hidden = times_transposed(pack_cotangent, wdown_back)
    grad_wdown = contract_rows(hidden_act, pack_cotangent)
    grad_gate = (grad_hidden * up_part * sigmoid_gate * (1.0 + gate * (1.0 - sigmoid_gate))).astype(
        jnp.bfloat16
    )
    grad_up = (grad_hidden * activated).astype(jnp.bfloat16)
    grad_wgate = contract_rows(pack_normed, grad_gate)
    grad_wup = contract_rows(pack_normed, grad_up)
    grad_normed_two = lax.psum_scatter(
        (times_transposed(grad_gate, wgate_back) + times_transposed(grad_up, wup_back)).astype(
            jnp.bfloat16
        ),
        "narrow",
        scatter_dimension=0,
        tiled=True,
    ).astype(jnp.float32)
    norm_two_back = jax.vjp(rms_scale, middle, gain_two)[1]
    grad_middle_norm, grad_gain_two = norm_two_back(grad_normed_two)
    grad_middle = cotangent.astype(jnp.float32) + grad_middle_norm
    grad_attn_proj = grad_middle.astype(jnp.bfloat16)
    grad_wout = contract_rows(attn_low, grad_attn_proj)
    attention_gradient = times_transposed(grad_attn_proj, wout_full).astype(jnp.bfloat16)
    head_gradients = attention_gradient.reshape(
        rows_per_shard, KEY_VALUE_HEADS, query_group, HEAD_WIDTH
    )
    delta = jnp.einsum(
        "tkgd,kgtd->kgt", head_gradients.astype(jnp.float32), attn_heads, precision=HIGHEST
    )

    def block_backward_pass(grad_query, inputs):
        key_block, value_block, doc_block, index_block = inputs
        probs = block_probs(key_block, doc_block, index_block)
        grad_probs = jnp.einsum(
            "tkgd,skd->kgts", head_gradients, value_block, preferred_element_type=jnp.float32
        )
        grad_scores = (probs * (grad_probs - delta[..., None])).astype(jnp.bfloat16)
        grad_query = (
            grad_query
            + jnp.einsum(
                "kgts,skd->tkgd", grad_scores, key_block, preferred_element_type=jnp.float32
            )
            * scale
        )
        grad_key = (
            jnp.einsum(
                "kgts,tkgd->skd", grad_scores, query_rows, preferred_element_type=jnp.float32
            )
            * scale
        )
        grad_value = jnp.einsum(
            "kgts,tkgd->skd",
            probs.astype(jnp.bfloat16),
            head_gradients,
            preferred_element_type=jnp.float32,
        )
        return (grad_query, (grad_key, grad_value))

    grad_query, (grad_key_blocks, grad_value_blocks) = lax.scan(
        block_backward_pass,
        jnp.zeros((rows_per_shard, KEY_VALUE_HEADS, query_group, HEAD_WIDTH), jnp.float32),
        input_per_block,
    )
    local_key_gradients, grad_values_local = (
        lax.psum_scatter(
            grad_key_blocks.reshape(pack_rows, key_total_width).astype(jnp.bfloat16),
            "narrow",
            scatter_dimension=0,
            tiled=True,
        ).astype(jnp.float32),
        lax.psum_scatter(
            grad_value_blocks.reshape(pack_rows, key_total_width).astype(jnp.bfloat16),
            "narrow",
            scatter_dimension=0,
            tiled=True,
        ).astype(jnp.float32),
    )
    grad_pre_query = query_back(grad_query.reshape(rows_per_shard, QUERY_HEADS, HEAD_WIDTH))[0]
    unrotated_key_gradient = key_backward(
        local_key_gradients.reshape(rows_per_shard, KEY_VALUE_HEADS, HEAD_WIDTH)
    )[0]
    grad_pre = jnp.concatenate(
        [
            grad_pre_query.reshape(rows_per_shard, query_total_width),
            unrotated_key_gradient.reshape(rows_per_shard, key_total_width),
            grad_values_local,
        ],
        axis=1,
    ).astype(jnp.bfloat16)
    grad_bias = jnp.sum(grad_pre.astype(jnp.float32), axis=0)
    grad_wqkv = contract_rows(normed_one, grad_pre)
    grad_normed_one = times_transposed(grad_pre, wqkv_full)
    norm_one_back = jax.vjp(rms_scale, hidden_in, gain_one)[1]
    grad_input_norm, grad_gain_one = norm_one_back(grad_normed_one)
    grad_input = grad_middle + grad_input_norm
    sum_wqkv, sum_bias, sum_wout, sum_gain_one, sum_gain_two = (
        lax.psum_scatter(grad_wqkv, ("wide", "narrow"), scatter_dimension=0, tiled=True),
        lax.psum_scatter(grad_bias, ("wide", "narrow"), scatter_dimension=0, tiled=True),
        lax.psum_scatter(grad_wout, ("wide", "narrow"), scatter_dimension=1, tiled=True),
        lax.psum_scatter(grad_gain_one, ("wide", "narrow"), scatter_dimension=0, tiled=True),
        lax.psum_scatter(grad_gain_two, ("wide", "narrow"), scatter_dimension=0, tiled=True),
    )
    sum_wgate, sum_wup, sum_wdown = (
        lax.psum_scatter(
            grad_wgate.astype(jnp.bfloat16), "wide", scatter_dimension=0, tiled=True
        ).astype(jnp.float32),
        lax.psum_scatter(
            grad_wup.astype(jnp.bfloat16), "wide", scatter_dimension=0, tiled=True
        ).astype(jnp.float32),
        lax.psum_scatter(
            grad_wdown.astype(jnp.bfloat16), "wide", scatter_dimension=1, tiled=True
        ).astype(jnp.float32),
    )
    return (
        layer_out[None],
        grad_input[None],
        sum_wqkv,
        sum_bias,
        sum_wout,
        sum_gain_one,
        sum_gain_two,
        sum_wgate,
        sum_wup,
        sum_wdown,
    )


def solution(mesh):
    placed = (
        P("wide", "narrow", None),
        P("wide", None),
        P(("wide", "narrow"), None),
        P(("wide", "narrow")),
        P(None, ("wide", "narrow")),
        P(("wide", "narrow")),
        P(("wide", "narrow")),
        P("wide", "narrow"),
        P("wide", "narrow"),
        P("narrow", "wide"),
        P("wide", "narrow", None),
    )
    return jax.shard_map(
        shards,
        mesh=mesh,
        in_specs=placed,
        out_specs=(
            P("wide", "narrow", None),
            P("wide", "narrow", None),
            P(("wide", "narrow"), None),
            P(("wide", "narrow")),
            P(None, ("wide", "narrow")),
            P(("wide", "narrow")),
            P(("wide", "narrow")),
            P("wide", "narrow"),
            P("wide", "narrow"),
            P("narrow", "wide"),
        ),
        check_vma=False,
    )
```

profile of v0, /device:TPU:0, one launch (start us, length us, event | category | flops | bytes accessed | tf_op | source)
XLA Modules:
  0.0 1367.8 jit_solution(4092313823965801265)
XLA Ops:
  12.0 42.5 %all-reduce.11 = (bf16[2048]{0:T(1024)(128)(2,1)S(1)}, bf16[1536]{0:T(1024)(128)(2,1)S(1)}, bf16[1536]{0:T(1024)(128)(2,1)S(1)}) all-reduce(bf16[2048]{0:T(1024)(128)(2,1)S(1)} %dynamic-update-slice.1, bf16[1536]{0:T(1024)(128)(2,1)S(1)} %dynamic-update-slice, ...), channel_id=1, replica_groups=mesh['wide'=8,'narrow'=4] {'wide','narrow'}, use_global_device_ids=true, to_apply=%add.5 | all-reduce | flops 5120 | bytes 20480
  58.7 24.4 %all-gather.9.cloned.1.call-done = bf16[1536,2048]{1,0:T(8,128)(2,1)} async-done(((bf16[48,2048]{1,0:T(8,128)(2,1)}), bf16[1536,2048]{1,0:T(8,128)(2,1)}) %all-gather.9.cloned.1.call-update) | async-done | bytes 6291472 | tf_op jit(solution)/shard_map/all_gather | solution.py:81
  108.1 40.1 %all-gather.11.cloned.1.call-done = bf16[1536,1536]{0,1:T(8,128)(2,1)} async-done(((bf16[1536,48]{0,1:T(8,128)(2,1)}), bf16[1536,1536]{0,1:T(8,128)(2,1)}) %all-gather.11.cloned.1.call-update) | async-done | bytes 4718608 | tf_op jit(solution)/shard_map/all_gather | solution.py:83
  156.5 100.5 %all-gather.15.cloned.1.call-done = bf16[1536,2240]{1,0:T(8,128)(2,1)} async-done(((bf16[192,2240]{1,0:T(8,128)(2,1)}), bf16[1536,2240]{1,0:T(8,128)(2,1)}) %all-gather.15.cloned.1.call-update) | async-done | bytes 6881296 | tf_op jit(solution)/shard_map/all_gather | solution.py:88
  257.0 19.8 %all-gather.13.cloned.1.call-done = bf16[512,1536]{1,0:T(8,128)(2,1)} async-done(((bf16[128,1536]{1,0:T(8,128)(2,1)}), bf16[512,1536]{1,0:T(8,128)(2,1)}) %all-gather.13.cloned.1.call-update) | async-done | bytes 1572880 | tf_op jit(solution)/shard_map/all_gather | solution.py:183
  276.8 9.5 fusion.47
  286.3 100.9 %all-gather.17.cloned.1.call-done = bf16[1536,2240]{1,0:T(8,128)(2,1)} async-done(((bf16[192,2240]{1,0:T(8,128)(2,1)}), bf16[1536,2240]{1,0:T(8,128)(2,1)}) %all-gather.17.cloned.1.call-update) | async-done | bytes 6881296 | tf_op jit(solution)/shard_map/all_gather | solution.py:89
  387.2 9.3 fusion.48
  396.5 9.9 all-gather.21.cloned.1.call-done
  406.5 110.5 %all-gather.19.cloned.1.call-done = bf16[2240,1536]{0,1:T(8,128)(2,1)} async-done(((bf16[2240,192]{0,1:T(8,128)(2,1)}), bf16[2240,1536]{0,1:T(8,128)(2,1)}) %all-gather.19.cloned.1.call-update) | async-done | bytes 6881296 | tf_op jit(solution)/shard_map/all_gather | solution.py:90
  517.0 13.3 multiply_convert_fusion
  530.3 7.8 fusion.49
  543.3 8.8 convolution_convert_fusion.3
  552.5 17.1 %reduce-scatter.16.cloned.1.call-done = bf16[128,1536]{1,0:T(8,128)(2,1)} async-done(((bf16[512,1536]{1,0:T(8,128)(2,1)}), bf16[128,1536]{1,0:T(8,128)(2,1)}) %reduce-scatter.16.cloned.1.call-update) | async-done | bytes 393232 | tf_op jit(solution)/shard_map/reduce_scatter | solution.py:211
  572.8 27.9 %reduce-scatter.14.cloned.1.call-done = bf16[128,1536]{1,0:T(8,128)(2,1)} async-done(((bf16[512,1536]{1,0:T(8,128)(2,1)}), bf16[128,1536]{1,0:T(8,128)(2,1)}) %reduce-scatter.14.cloned.1.call-update) | async-done | bytes 393232 | tf_op jit(solution)/shard_map/reduce_scatter | solution.py:189
  622.7 8.9 convolution_convert_fusion.2
  633.1 7.6 convolution_convert_fusion.1
  642.1 7.5 convolution_convert_fusion
  674.3 43.1 %all-reduce.10 = (f32[2048]{0:T(1024)S(1)}, f32[1536]{0:T(1024)S(1)}, f32[1536]{0:T(1024)S(1)}) all-reduce(f32[2048]{0:T(1024)S(1)} %convert_reduce_fusion, f32[1536]{0:T(1024)S(1)} %get-tuple-element.83, f32[1536]{0:T(1024)S(1)} %copy-done.22), channel_id=8, replica_groups=mesh['wide'=8,'narrow'=4] {'wide','narrow'}, use_global_device_ids=true, to_apply=%region_16.17.clone | all-reduce | flops 5120 | bytes 40960
  720.3 75.0 %reduce-scatter.22.cloned.1.call-done = bf16[192,2240]{1,0:T(8,128)(2,1)} async-done(((bf16[1536,2240]{1,0:T(8,128)(2,1)}), bf16[192,2240]{1,0:T(8,128)(2,1)}) %reduce-scatter.22.cloned.1.call-update) | async-done | bytes 860176 | tf_op jit(solution)/shard_map/reduce_scatter | solution.py:305
  797.8 129.5 %reduce-scatter.24.cloned.1.call-done = bf16[192,2240]{1,0:T(8,128)(2,1)} async-done(((bf16[1536,2240]{1,0:T(8,128)(2,1)}), bf16[192,2240]{1,0:T(8,128)(2,1)}) %reduce-scatter.24.cloned.1.call-update) | async-done | bytes 860176 | tf_op jit(solution)/shard_map/reduce_scatter | solution.py:308
  929.8 129.4 %reduce-scatter.26.cloned.1.call-done = bf16[2240,192]{0,1:T(8,128)(2,1)} async-done(((bf16[2240,1536]{0,1:T(8,128)(2,1)}), bf16[2240,192]{0,1:T(8,128)(2,1)}) %reduce-scatter.26.cloned.1.call-update) | async-done | bytes 860176 | tf_op jit(solution)/shard_map/reduce_scatter | solution.py:311
  1061.6 139.1 %reduce-scatter.20.cloned.1.call-done = f32[1536,48]{0,1:T(8,128)} async-done(((f32[1536,1536]{0,1:T(8,128)}), f32[1536,48]{0,1:T(8,128)}) %reduce-scatter.20.cloned.1.call-update) | async-done | bytes 294928 | tf_op jit(solution)/shard_map/reduce_scatter | solution.py:300
  1200.8 160.3 %reduce-scatter.18.cloned.1.call-done = f32[48,2048]{1,0:T(8,128)} async-done(((f32[1536,2048]{1,0:T(8,128)}), f32[48,2048]{1,0:T(8,128)}) %reduce-scatter.18.cloned.1.call-update) | async-done | bytes 393232 | tf_op jit(solution)/shard_map/reduce_scatter | solution.py:298
  (191 shorter events, 110.2 us)
Async XLA Ops:
  7.2 75.9 %all-gather.9.cloned.1.call-start = ((), (), s32[]{:S(2)}) async-start(), calls=%async_computation.9 | async-start | bytes 6488064 | tf_op jit(solution)/shard_map/all_gather | solution.py:81
  7.9 140.3 %all-gather.11.cloned.1.call-start = ((), (), s32[]{:S(2)}) async-start(), calls=%async_computation.10 | async-start | bytes 4866048 | tf_op jit(solution)/shard_map/all_gather | solution.py:83
  8.7 248.4 %all-gather.15.cloned.1.call-start = ((), (), s32[]{:S(2)}) async-start(), calls=%async_computation.12 | async-start | bytes 7962624 | tf_op jit(solution)/shard_map/all_gather | solution.py:88
  9.4 267.4 %all-gather.13.cloned.1.call-start = ((), (), s32[]{:S(2)}) async-start(), calls=%async_computation.11 | async-start | bytes 1966080 | tf_op jit(solution)/shard_map/all_gather | solution.py:183
  56.5 31.0 %copy-start.12 = (f32[128,64]{1,0:T(8,128)}, f32[128,64]{1,0:T(8,128)S(1)}, u32[]{:S(2)}) copy-start(f32[128,64]{1,0:T(8,128)S(1)} %get-tuple-element.136) | copy-start | bytes 98308
  56.5 31.0 %copy-start.14 = (f32[128,64]{1,0:T(8,128)}, f32[128,64]{1,0:T(8,128)S(1)}, u32[]{:S(2)}) copy-start(f32[128,64]{1,0:T(8,128)S(1)} %get-tuple-element.137) | copy-start | bytes 98308
  56.6 31.5 %copy-start.17 = (f32[128,64]{0,1:T(8,128)}, f32[128,64]{0,1:T(8,128)S(1)}, u32[]{:S(2)}) copy-start(f32[128,64]{0,1:T(8,128)S(1)} %copy.113) | copy-start | bytes 98308
  56.7 31.4 %copy-start.19 = (f32[128,64]{0,1:T(8,128)}, f32[128,64]{0,1:T(8,128)S(1)}, u32[]{:S(2)}) copy-start(f32[128,64]{0,1:T(8,128)S(1)} %copy.114) | copy-start | bytes 98308
  57.9 25.2 %copy-start.28 = (f32[128]{0:T(128)}, f32[128]{0:T(128)S(1)}, u32[]{:S(2)}) copy-start(f32[128]{0:T(128)S(1)} %fusion.23) | copy-start | bytes 1540
  58.0 25.1 %copy-start.23 = (f32[128]{0:T(128)}, f32[128]{0:T(128)S(1)}, u32[]{:S(2)}) copy-start(f32[128]{0:T(128)S(1)} %fusion.36) | copy-start | bytes 1540
  105.5 42.6 %copy-start.3 = (bf16[1,128,1536]{2,1,0:T(8,128)(2,1)S(1)}, bf16[1,128,1536]{2,1,0:T(8,128)(2,1)}, u32[]{:S(2)}) copy-start(bf16[1,128,1536]{2,1,0:T(8,128)(2,1)} %param.11) | copy-start | bytes 1179652
  154.3 232.9 %all-gather.17.cloned.1.call-start = ((), (), s32[]{:S(2)}) async-start(), calls=%async_computation.13 | async-start | bytes 7962624 | tf_op jit(solution)/shard_map/all_gather | solution.py:89
  154.9 251.5 %all-gather.21.cloned.1.call-start = ((), (), s32[]{:S(2)}) async-start(), calls=%async_computation.22 | async-start | bytes 1966080 | tf_op jit(solution)/shard_map/all_gather | solution.py:202
  155.5 361.5 %all-gather.19.cloned.1.call-start = ((), (), s32[]{:S(2)}) async-start(), calls=%async_computation.14 | async-start | bytes 7962624 | tf_op jit(solution)/shard_map/all_gather | solution.py:90
  156.3 413.3 %reduce-scatter.16.cloned.1.call-start = ((), (), s32[]{:S(2)}) async-start(), calls=%async_computation.16 | async-start | bytes 1966080 | tf_op jit(solution)/shard_map/reduce_scatter | solution.py:211
  543.2 57.6 %reduce-scatter.14.cloned.1.call-start = ((), (), s32[]{:S(2)}) async-start(), calls=%async_computation.15 | async-start | bytes 1966080 | tf_op jit(solution)/shard_map/reduce_scatter | solution.py:189
  552.0 105.9 %reduce-scatter.28.cloned.1.call-start = ((), (), s32[]{:S(2)}) async-start(), calls=%async_computation.23 | async-start | bytes 327680
  618.2 43.4 %reduce-scatter.30.cloned.1.call-start = ((), (), s32[]{:S(2)}) async-start(), calls=%async_computation.24 | async-start | bytes 327680
  622.7 172.6 %reduce-scatter.22.cloned.1.call-start = ((), (), s32[]{:S(2)}) async-start(), calls=%async_computation.19 | async-start | bytes 7962624 | tf_op jit(solution)/shard_map/reduce_scatter | solution.py:305
  631.7 295.6 %reduce-scatter.24.cloned.1.call-start = ((), (), s32[]{:S(2)}) async-start(), calls=%async_computation.20 | async-start | bytes 7962624 | tf_op jit(solution)/shard_map/reduce_scatter | solution.py:308
  640.7 418.5 %reduce-scatter.26.cloned.1.call-start = ((), (), s32[]{:S(2)}) async-start(), calls=%async_computation.21 | async-start | bytes 7962624 | tf_op jit(solution)/shard_map/reduce_scatter | solution.py:311
  649.6 551.1 %reduce-scatter.20.cloned.1.call-start = ((), (), s32[]{:S(2)}) async-start(), calls=%async_computation.18 | async-start | bytes 9732096 | tf_op jit(solution)/shard_map/reduce_scatter | solution.py:300
  655.9 705.1 %reduce-scatter.18.cloned.1.call-start = ((), (), s32[]{:S(2)}) async-start(), calls=%async_computation.17 | async-start | bytes 12976128 | tf_op jit(solution)/shard_map/reduce_scatter | solution.py:298
  669.2 50.0 %copy-start.29 = (f32[128]{0:T(128)S(1)}, f32[128]{0:T(128)}, u32[]{:S(2)}) copy-start(f32[128]{0:T(128)} %copy-done.28) | copy-start | bytes 1540
  (28 other events, 98.0 us)
Sparse Core Ops, SparseCore 0:
  10.8 72.2 all-gather.8
  86.0 62.1 all-gather.10
  150.4 106.5 all-gather.14
  259.0 17.7 all-gather.12
  278.9 108.2 all-gather.16
  388.6 17.7 all-gather.20
  408.6 108.2 all-gather.18
  543.3 26.2 reduce-scatter.15
  572.7 28.0 reduce-scatter.13
  618.3 20.0 reduce-scatter.27
  641.4 20.0 reduce-scatter.29
  665.1 130.1 reduce-scatter.21
  799.0 128.2 reduce-scatter.23
  930.8 128.2 reduce-scatter.25
  1065.4 135.2 reduce-scatter.19
  1207.2 153.7 reduce-scatter.17
where the time goes:
time: 1380 us; the launch traced here: 1370 us
  waiting for transfers between devices  1090 us (79%)
  matrix products  117 us (8%)
  blocking collectives  97.3 us (7%)
  local copies, waits for them, and re-layouts  23.7 us (2%)
  other arithmetic  23 us (2%)
  between operations  14.7 us (1%)
    reduce_scatter x1, waiting for transfers between devices, shards(): lax.psum_scatter(grad_wqkv, ('wide', 'narrow'), scatter_dimension=0, tile...  160 us
    reduce_scatter x1, waiting for transfers between devices, shards(): lax.psum_scatter(grad_wout, ('wide', 'narrow'), scatter_dimension=1, tile...  139 us
    reduce_scatter x1, waiting for transfers between devices, shards(): lax.psum_scatter(grad_wup.astype(jnp.bfloat16), 'wide', scatter_dimension...  130 us
    reduce_scatter x1, waiting for transfers between devices, shards(): lax.psum_scatter(grad_wdown.astype(jnp.bfloat16), 'wide', scatter_dimensi...  129 us
    all_gather x1, waiting for transfers between devices, shards(): lax.all_gather(w_down, 'wide', axis=1, tiled=True)  111 us
    all_gather x1, waiting for transfers between devices, shards(): lax.all_gather(w_up, 'wide', axis=0, tiled=True)  101 us
    all_gather x1, waiting for transfers between devices, shards(): lax.all_gather(w_gate, 'wide', axis=0, tiled=True)  101 us
    unnamed x2, blocking collectives  85.6 us
  transfers between devices with their start and end apart: 16, of which 15 were waited for; matrix products, arithmetic and copies ran while one was open for 8% of the time, Pallas kernels for 0%

commit v1 on v0

--- a/solution.py
+++ b/solution.py
@@ -11,6 +11,19 @@
 ROPE_BASE = 10000.0
 NEGATIVE_BIG = -1e30
 HIGHEST = lax.Precision.HIGHEST
+
+
+def gather_around(x, axis, dim):
+    length, index, rows = (lax.axis_size(axis), lax.axis_index(axis), x.shape[dim])
+    forward = [(i, (i + 1) % length) for i in range(length)]
+    whole = jnp.zeros((*x.shape[:dim], length * rows, *x.shape[dim + 1 :]), x.dtype)
+    held = x
+    for step in range(length):
+        owner = (index - step) % length
+        whole = lax.dynamic_update_slice_in_dim(whole, held, owner * rows, axis=dim)
+        if step < length - 1:
+            held = lax.ppermute(held, axis, forward)
+    return whole
 
 
 def rms_scale(value_rows, gain):
@@ -86,7 +99,7 @@
     )
     wgate_full, wup_full, wdown_full = (
         lax.all_gather(w_gate, "wide", axis=0, tiled=True),
-        lax.all_gather(w_up, "wide", axis=0, tiled=True),
+        gather_around(w_up, "wide", 0),
         lax.all_gather(w_down, "wide", axis=1, tiled=True),
     )
     gain_one = gain_one.astype(jnp.float32)

time: 1380 us -> 1450 us (1.051)
  waiting for transfers between devices: 1090 us -> 1140 us
  local copies, waits for them, and re-layouts: 23.7 us -> 41.5 us
    ppermute x0 -> x7, waiting for transfers between devices: none -> 243 us  [gather_around(): held = lax.ppermute(held, axis, forward)]
    all_gather x1, waiting for transfers between devices: 111 us -> 0.01 us  [shards(): lax.all_gather(w_down, 'wide', axis=1, tiled=True)]
    all_gather x1, waiting for transfers between devices: 101 us -> 52.1 us  [shards(): lax.all_gather(w_gate, 'wide', axis=0, tiled=True)]
    all_gather x1, waiting for transfers between devices: 101 us -> 78.1 us  [shards(): lax.all_gather(w_up, 'wide', axis=0, tiled=True)]
  transfers between devices with their start and end apart: 16 -> 23, of which waited for: 15 -> 20; matrix products, arithmetic and copies ran while one was open for 8% -> 10% of each run, Pallas kernels for 0% -> 0%
where the time goes in v1:
time: 1450 us; the launch traced here: 1440 us
  waiting for transfers between devices  1140 us (79%)
  matrix products  124 us (9%)
  blocking collectives  97.3 us (7%)
  local copies, waits for them, and re-layouts  41.5 us (3%)
  other arithmetic  22 us (2%)
  between operations  14.7 us (1%)
    ppermute x7, waiting for transfers between devices, gather_around(): held = lax.ppermute(held, axis, forward)  243 us
    reduce_scatter x1, waiting for transfers between devices, shards(): lax.psum_scatter(grad_wqkv, ('wide', 'narrow'), scatter_dimension=0, tile...  160 us
    reduce_scatter x1, waiting for transfers between devices, shards(): lax.psum_scatter(grad_wout, ('wide', 'narrow'), scatter_dimension=1, tile...  139 us
    reduce_scatter x1, waiting for transfers between devices, shards(): lax.psum_scatter(grad_wup.astype(jnp.bfloat16), 'wide', scatter_dimension...  130 us
    reduce_scatter x1, waiting for transfers between devices, shards(): lax.psum_scatter(grad_wdown.astype(jnp.bfloat16), 'wide', scatter_dimensi...  129 us
    unnamed x2, blocking collectives  85.5 us
    all_gather x1, waiting for transfers between devices, shards(): lax.all_gather(w_up, 'wide', axis=0, tiled=True)  78.1 us
    reduce_scatter x1, waiting for transfers between devices, shards(): lax.psum_scatter(grad_wgate.astype(jnp.bfloat16), 'wide', scatter_dimensi...  75 us
  transfers between devices with their start and end apart: 23, of which 20 were waited for; matrix products, arithmetic and copies ran while one was open for 10% of the time, Pallas kernels for 0%

profile of v1, /device:TPU:0, one launch (start us, length us, event | category | flops | bytes accessed | tf_op | source)
XLA Modules:
  0.0 1441.9 jit_solution(9255937782083285823)
XLA Ops:
  13.2 42.4 %all-reduce.11 = (bf16[2048]{0:T(1024)(128)(2,1)S(1)}, bf16[1536]{0:T(1024)(128)(2,1)S(1)}, bf16[1536]{0:T(1024)(128)(2,1)S(1)}) all-reduce(bf16[2048]{0:T(1024)(128)(2,1)S(1)} %dynamic-update-slice.1, bf16[1536]{0:T(1024)(128)(2,1)S(1)} %dynamic-update-slice, ...), channel_id=1, replica_groups=mesh['wide'=8,'narrow'=4] {'wide','narrow'}, use_global_device_ids=true, to_apply=%add.5 | all-reduce | flops 5120 | bytes 20480
  58.8 24.0 %all-gather.9.cloned.1.call-done = bf16[1536,2048]{1,0:T(8,128)(2,1)} async-done(((bf16[48,2048]{1,0:T(8,128)(2,1)}), bf16[1536,2048]{1,0:T(8,128)(2,1)}) %all-gather.9.cloned.1.call-update) | async-done | bytes 6291472 | tf_op jit(solution)/shard_map/all_gather | solution.py:94
  109.2 38.7 %all-gather.11.cloned.1.call-done = bf16[1536,1536]{0,1:T(8,128)(2,1)} async-done(((bf16[1536,48]{0,1:T(8,128)(2,1)}), bf16[1536,1536]{0,1:T(8,128)(2,1)}) %all-gather.11.cloned.1.call-update) | async-done | bytes 4718608 | tf_op jit(solution)/shard_map/all_gather | solution.py:96
  156.4 23.2 %collective-permute-done = bf16[192,2240]{1,0:T(8,128)(2,1)S(1)} collective-permute-done((bf16[192,2240]{1,0:T(8,128)(2,1)}, bf16[192,2240]{1,0:T(8,128)(2,1)S(1)}, u32[]{:S(2)}, u32[]{:S(2)}) %collective-permute-start) | collective-permute-done | bytes 860192 | tf_op jit(solution)/shard_map/ppermute | solution.py:25
  180.5 43.7 %collective-permute-done.1 = bf16[192,2240]{1,0:T(8,128)(2,1)S(1)} collective-permute-done((bf16[192,2240]{1,0:T(8,128)(2,1)S(1)}, bf16[192,2240]{1,0:T(8,128)(2,1)S(1)}, u32[]{:S(2)}, u32[]{:S(2)}) %collective-permute-start.1) | collective-permute-done | bytes 860192 | tf_op jit(solution)/shard_map/ppermute | solution.py:25
  225.1 34.1 %collective-permute-done.2 = bf16[192,2240]{1,0:T(8,128)(2,1)S(1)} collective-permute-done((bf16[192,2240]{1,0:T(8,128)(2,1)S(1)}, bf16[192,2240]{1,0:T(8,128)(2,1)S(1)}, u32[]{:S(2)}, u32[]{:S(2)}) %collective-permute-start.2) | collective-permute-done | bytes 860192 | tf_op jit(solution)/shard_map/ppermute | solution.py:25
  260.1 43.3 %collective-permute-done.3 = bf16[192,2240]{1,0:T(8,128)(2,1)} collective-permute-done((bf16[192,2240]{1,0:T(8,128)(2,1)S(1)}, bf16[192,2240]{1,0:T(8,128)(2,1)}, u32[]{:S(2)}, u32[]{:S(2)}) %collective-permute-start.3) | collective-permute-done | bytes 860192 | tf_op jit(solution)/shard_map/ppermute | solution.py:25
  307.8 37.1 %collective-permute-done.4 = bf16[192,2240]{1,0:T(8,128)(2,1)} collective-permute-done((bf16[192,2240]{1,0:T(8,128)(2,1)}, bf16[192,2240]{1,0:T(8,128)(2,1)}, u32[]{:S(2)}, u32[]{:S(2)}) %collective-permute-start.4) | collective-permute-done | bytes 860192 | tf_op jit(solution)/shard_map/ppermute | solution.py:25
  347.8 32.2 %collective-permute-done.5 = bf16[192,2240]{1,0:T(8,128)(2,1)S(1)} collective-permute-done((bf16[192,2240]{1,0:T(8,128)(2,1)}, bf16[192,2240]{1,0:T(8,128)(2,1)S(1)}, u32[]{:S(2)}, u32[]{:S(2)}) %collective-permute-start.5) | collective-permute-done | bytes 860192 | tf_op jit(solution)/shard_map/ppermute | solution.py:25
  385.6 29.2 %collective-permute-done.6 = bf16[192,2240]{1,0:T(8,128)(2,1)S(1)} collective-permute-done((bf16[192,2240]{1,0:T(8,128)(2,1)S(1)}, bf16[192,2240]{1,0:T(8,128)(2,1)S(1)}, u32[]{:S(2)}, u32[]{:S(2)}) %collective-permute-start.6) | collective-permute-done | bytes 860192 | tf_op jit(solution)/shard_map/ppermute | solution.py:25
  425.2 52.1 %all-gather.15.cloned.1.call-done = bf16[1536,2240]{1,0:T(8,128)(2,1)} async-done(((bf16[192,2240]{1,0:T(8,128)(2,1)}), bf16[1536,2240]{1,0:T(8,128)(2,1)}) %all-gather.15.cloned.1.call-update) | async-done | bytes 6881296 | tf_op jit(solution)/shard_map/all_gather | solution.py:101
  477.3 19.8 %all-gather.13.cloned.1.call-done = bf16[512,1536]{1,0:T(8,128)(2,1)} async-done(((bf16[128,1536]{1,0:T(8,128)(2,1)}), bf16[512,1536]{1,0:T(8,128)(2,1)}) %all-gather.13.cloned.1.call-update) | async-done | bytes 1572880 | tf_op jit(solution)/shard_map/all_gather | solution.py:196
  497.2 9.6 fusion.47
  506.8 13.6 multiply_convert_fusion
  529.6 78.1 %all-gather.19.cloned.1.call-done = bf16[1536,2240]{1,0:T(8,128)(2,1)} async-done(((bf16[192,2240]{1,0:T(8,128)(2,1)}), bf16[1536,2240]{1,0:T(8,128)(2,1)}) %all-gather.19.cloned.1.call-update) | async-done | bytes 6881296 | tf_op jit(solution)/shard_map/all_gather | solution.py:211
  607.7 9.6 fusion.3
  626.8 16.9 %reduce-scatter.16.cloned.1.call-done = bf16[128,1536]{1,0:T(8,128)(2,1)} async-done(((bf16[512,1536]{1,0:T(8,128)(2,1)}), bf16[128,1536]{1,0:T(8,128)(2,1)}) %reduce-scatter.16.cloned.1.call-update) | async-done | bytes 393232 | tf_op jit(solution)/shard_map/reduce_scatter | solution.py:224
  646.9 27.9 %reduce-scatter.14.cloned.1.call-done = bf16[128,1536]{1,0:T(8,128)(2,1)} async-done(((bf16[512,1536]{1,0:T(8,128)(2,1)}), bf16[128,1536]{1,0:T(8,128)(2,1)}) %reduce-scatter.14.cloned.1.call-update) | async-done | bytes 393232 | tf_op jit(solution)/shard_map/reduce_scatter | solution.py:202
  748.4 43.1 %all-reduce.10 = (f32[2048]{0:T(1024)S(1)}, f32[1536]{0:T(1024)S(1)}, f32[1536]{0:T(1024)S(1)}) all-reduce(f32[2048]{0:T(1024)S(1)} %convert_reduce_fusion, f32[1536]{0:T(1024)S(1)} %get-tuple-element.83, f32[1536]{0:T(1024)S(1)} %copy-done.28), channel_id=8, replica_groups=mesh['wide'=8,'narrow'=4] {'wide','narrow'}, use_global_device_ids=true, to_apply=%region_16.17.clone | all-reduce | flops 5120 | bytes 40960
  794.4 75.0 %reduce-scatter.22.cloned.1.call-done = bf16[192,2240]{1,0:T(8,128)(2,1)} async-done(((bf16[1536,2240]{1,0:T(8,128)(2,1)}), bf16[192,2240]{1,0:T(8,128)(2,1)}) %reduce-scatter.22.cloned.1.call-update) | async-done | bytes 860176 | tf_op jit(solution)/shard_map/reduce_scatter | solution.py:318
  871.9 129.5 %reduce-scatter.24.cloned.1.call-done = bf16[192,2240]{1,0:T(8,128)(2,1)} async-done(((bf16[1536,2240]{1,0:T(8,128)(2,1)}), bf16[192,2240]{1,0:T(8,128)(2,1)}) %reduce-scatter.24.cloned.1.call-update) | async-done | bytes 860176 | tf_op jit(solution)/shard_map/reduce_scatter | solution.py:321
  1003.8 129.4 %reduce-scatter.26.cloned.1.call-done = bf16[2240,192]{0,1:T(8,128)(2,1)} async-done(((bf16[2240,1536]{0,1:T(8,128)(2,1)}), bf16[2240,192]{0,1:T(8,128)(2,1)}) %reduce-scatter.26.cloned.1.call-update) | async-done | bytes 860176 | tf_op jit(solution)/shard_map/reduce_scatter | solution.py:324
  1135.7 139.2 %reduce-scatter.20.cloned.1.call-done = f32[1536,48]{0,1:T(8,128)} async-done(((f32[1536,1536]{0,1:T(8,128)}), f32[1536,48]{0,1:T(8,128)}) %reduce-scatter.20.cloned.1.call-update) | async-done | bytes 294928 | tf_op jit(solution)/shard_map/reduce_scatter | solution.py:313
  1274.9 160.2 %reduce-scatter.18.cloned.1.call-done = f32[48,2048]{1,0:T(8,128)} async-done(((f32[1536,2048]{1,0:T(8,128)}), f32[48,2048]{1,0:T(8,128)}) %reduce-scatter.18.cloned.1.call-update) | async-done | bytes 393232 | tf_op jit(solution)/shard_map/reduce_scatter | solution.py:311
  (224 shorter events, 175.3 us)
Async XLA Ops:
  7.2 50.7 %copy-start.3 = (bf16[1,128,1536]{2,1,0:T(8,128)(2,1)S(1)}, bf16[1,128,1536]{2,1,0:T(8,128)(2,1)}, u32[]{:S(2)}) copy-start(bf16[1,128,1536]{2,1,0:T(8,128)(2,1)} %param.11) | copy-start | bytes 1179652
  7.2 75.6 %all-gather.9.cloned.1.call-start = ((), (), s32[]{:S(2)}) async-start(), calls=%async_computation.9 | async-start | bytes 6488064 | tf_op jit(solution)/shard_map/all_gather | solution.py:94
  7.9 140.0 %all-gather.11.cloned.1.call-start = ((), (), s32[]{:S(2)}) async-start(), calls=%async_computation.10 | async-start | bytes 4866048 | tf_op jit(solution)/shard_map/all_gather | solution.py:96
  8.7 407.1 %all-gather.21.cloned.1.call-start = ((), (), s32[]{:S(2)}) async-start(), calls=%async_computation.22 | async-start | bytes 1966080 | tf_op jit(solution)/shard_map/all_gather | solution.py:215
  9.4 406.3 %all-gather.17.cloned.1.call-start = ((), (), s32[]{:S(2)}) async-start(), calls=%async_computation.13 | async-start | bytes 7962624 | tf_op jit(solution)/shard_map/all_gather | solution.py:103
  10.0 467.4 %all-gather.15.cloned.1.call-start = ((), (), s32[]{:S(2)}) async-start(), calls=%async_computation.12 | async-start | bytes 7962624 | tf_op jit(solution)/shard_map/all_gather | solution.py:101
  10.6 486.6 %all-gather.13.cloned.1.call-start = ((), (), s32[]{:S(2)}) async-start(), calls=%async_computation.11 | async-start | bytes 1966080 | tf_op jit(solution)/shard_map/all_gather | solution.py:196
  154.0 453.6 %all-gather.19.cloned.1.call-start = ((), (), s32[]{:S(2)}) async-start(), calls=%async_computation.15 | async-start | bytes 7962624 | tf_op jit(solution)/shard_map/all_gather | solution.py:211
  154.8 488.9 %reduce-scatter.16.cloned.1.call-start = ((), (), s32[]{:S(2)}) async-start(), calls=%async_computation.16 | async-start | bytes 1966080 | tf_op jit(solution)/shard_map/reduce_scatter | solution.py:224
  154.8 24.8 %collective-permute-start = (bf16[192,2240]{1,0:T(8,128)(2,1)}, bf16[192,2240]{1,0:T(8,128)(2,1)S(1)}, u32[]{:S(2)}, u32[]{:S(2)}) collective-permute-start(bf16[192,2240]{1,0:T(8,128)(2,1)} %param.19), channel_id=1, source_target_pairs={{0,4},{4,8},{8,12},{12,16},{16,20},{20,24},{24,28},{28,0},{1,5},{5... | collective-permute-start | bytes 2580488 | tf_op jit(solution)/shard_map/ppermute | solution.py:25
  180.5 43.7 %collective-permute-start.1 = (bf16[192,2240]{1,0:T(8,128)(2,1)S(1)}, bf16[192,2240]{1,0:T(8,128)(2,1)S(1)}, u32[]{:S(2)}, u32[]{:S(2)}) collective-permute-start(bf16[192,2240]{1,0:T(8,128)(2,1)S(1)} %collective-permute-done), channel_id=1, source_target_pairs={{0,4},{4,8},{8,12},{12,16},{16,20},{20,24},{24,28},{28,0},{1,5},{5... | collective-permute-start | bytes 2580488 | tf_op jit(solution)/shard_map/ppermute | solution.py:25
  225.1 34.1 %collective-permute-start.2 = (bf16[192,2240]{1,0:T(8,128)(2,1)S(1)}, bf16[192,2240]{1,0:T(8,128)(2,1)S(1)}, u32[]{:S(2)}, u32[]{:S(2)}) collective-permute-start(bf16[192,2240]{1,0:T(8,128)(2,1)S(1)} %collective-permute-done.1), channel_id=1, source_target_pairs={{0,4},{4,8},{8,12},{12,16},{16,20},{20,24},{24,28},{28,0},{1,5},{5... | collective-permute-start | bytes 2580488 | tf_op jit(solution)/shard_map/ppermute | solution.py:25
  260.1 43.3 %collective-permute-start.3 = (bf16[192,2240]{1,0:T(8,128)(2,1)S(1)}, bf16[192,2240]{1,0:T(8,128)(2,1)}, u32[]{:S(2)}, u32[]{:S(2)}) collective-permute-start(bf16[192,2240]{1,0:T(8,128)(2,1)S(1)} %collective-permute-done.2), channel_id=1, source_target_pairs={{0,4},{4,8},{8,12},{12,16},{16,20},{20,24},{24,28},{28,0},{1,5},{5... | collective-permute-start | bytes 2580488 | tf_op jit(solution)/shard_map/ppermute | solution.py:25
  303.4 41.5 %collective-permute-start.4 = (bf16[192,2240]{1,0:T(8,128)(2,1)}, bf16[192,2240]{1,0:T(8,128)(2,1)}, u32[]{:S(2)}, u32[]{:S(2)}) collective-permute-start(bf16[192,2240]{1,0:T(8,128)(2,1)} %collective-permute-done.3), channel_id=1, source_target_pairs={{0,4},{4,8},{8,12},{12,16},{16,20},{20,24},{24,28},{28,0},{1,5},{5... | collective-permute-start | bytes 2580488 | tf_op jit(solution)/shard_map/ppermute | solution.py:25
  344.9 35.1 %collective-permute-start.5 = (bf16[192,2240]{1,0:T(8,128)(2,1)}, bf16[192,2240]{1,0:T(8,128)(2,1)S(1)}, u32[]{:S(2)}, u32[]{:S(2)}) collective-permute-start(bf16[192,2240]{1,0:T(8,128)(2,1)} %collective-permute-done.4), channel_id=1, source_target_pairs={{0,4},{4,8},{8,12},{12,16},{16,20},{20,24},{24,28},{28,0},{1,5},{5... | collective-permute-start | bytes 2580488 | tf_op jit(solution)/shard_map/ppermute | solution.py:25
  380.0 34.7 %collective-permute-start.6 = (bf16[192,2240]{1,0:T(8,128)(2,1)S(1)}, bf16[192,2240]{1,0:T(8,128)(2,1)S(1)}, u32[]{:S(2)}, u32[]{:S(2)}) collective-permute-start(bf16[192,2240]{1,0:T(8,128)(2,1)S(1)} %collective-permute-done.5), channel_id=1, source_target_pairs={{0,4},{4,8},{8,12},{12,16},{16,20},{20,24},{24,28},{28,0},{1,5},{5... | collective-permute-start | bytes 2580488 | tf_op jit(solution)/shard_map/ppermute | solution.py:25
  617.3 57.5 %reduce-scatter.14.cloned.1.call-start = ((), (), s32[]{:S(2)}) async-start(), calls=%async_computation.14 | async-start | bytes 1966080 | tf_op jit(solution)/shard_map/reduce_scatter | solution.py:202
  626.7 105.2 %reduce-scatter.28.cloned.1.call-start = ((), (), s32[]{:S(2)}) async-start(), calls=%async_computation.23 | async-start | bytes 327680
  692.2 43.4 %reduce-scatter.30.cloned.1.call-start = ((), (), s32[]{:S(2)}) async-start(), calls=%async_computation.24 | async-start | bytes 327680
  696.7 172.6 %reduce-scatter.22.cloned.1.call-start = ((), (), s32[]{:S(2)}) async-start(), calls=%async_computation.19 | async-start | bytes 7962624 | tf_op jit(solution)/shard_map/reduce_scatter | solution.py:318
  705.7 295.6 %reduce-scatter.24.cloned.1.call-start = ((), (), s32[]{:S(2)}) async-start(), calls=%async_computation.20 | async-start | bytes 7962624 | tf_op jit(solution)/shard_map/reduce_scatter | solution.py:321
  714.7 418.5 %reduce-scatter.26.cloned.1.call-start = ((), (), s32[]{:S(2)}) async-start(), calls=%async_computation.21 | async-start | bytes 7962624 | tf_op jit(solution)/shard_map/reduce_scatter | solution.py:324
  723.6 551.3 %reduce-scatter.20.cloned.1.call-start = ((), (), s32[]{:S(2)}) async-start(), calls=%async_computation.18 | async-start | bytes 9732096 | tf_op jit(solution)/shard_map/reduce_scatter | solution.py:313
  729.9 705.2 %reduce-scatter.18.cloned.1.call-start = ((), (), s32[]{:S(2)}) async-start(), calls=%async_computation.17 | async-start | bytes 12976128 | tf_op jit(solution)/shard_map/reduce_scatter | solution.py:311
  (40 other events, 422.0 us)
Sparse Core Ops, SparseCore 0:
  10.9 71.9 all-gather.8
  85.7 62.1 all-gather.10
  149.5 17.9 all-gather.20
  169.5 157.7 all-gather.16
  329.3 147.9 all-gather.14
  479.3 17.7 all-gather.12
  499.4 108.2 all-gather.18
  617.4 26.2 reduce-scatter.15
  646.8 27.9 reduce-scatter.13
  692.3 20.0 reduce-scatter.27
  715.5 20.0 reduce-scatter.29
  739.1 130.2 reduce-scatter.21
  873.0 128.2 reduce-scatter.23
  1004.9 128.2 reduce-scatter.25
  1139.5 135.3 reduce-scatter.19
  1281.4 153.7 reduce-scatter.17
